TPU v7x, 256 devices: a whole 4x4x8 slice. The times are simulated.
256 devices in a mesh: fsdp: 8 (over x, core), vocab: 32 (over y, z).
Axes of the slice: x: 4, y: 4, z: 8, core: 2. Of those that a mesh axis runs over, the one named last changes fastest.
Arguments:
- hidden_states: bfloat16 [1024, 3072], P('fsdp', 'vocab'), may hold values from -512 to 512
- head: bfloat16 [3072, 65536], P('fsdp', 'vocab'), may hold values from -0.25259074 to 0.25259074
- labels: int32 [1024], P('fsdp'), may hold values from 0 to 65535
Outputs:
- token_loss: float32 [1024], P('fsdp')
- state_grad: bfloat16 [1024, 3072], P('fsdp', 'vocab')
- head_grad: float32 [3072, 65536], P('fsdp', 'vocab')
All inputs are finite; a program needn't handle non-finite values.
Results may differ from a plain program's by a relative error of at most 0.0034.
Values may be sent and summed in bfloat16 or wider, within the bound.
A program may use at most 128 MiB of HBM per device.

v0:
```python
import jax
import jax.numpy as jnp
from jax import lax
from jax.sharding import PartitionSpec as P


def combine(stats):
    peaks, totals, targets = (stats[:, 0], stats[:, 1], stats[:, 2])
    peak = jnp.max(peaks, axis=0)
    total = jnp.sum(totals * jnp.exp(peaks - peak[None]), axis=0)
    return jnp.stack([peak, total, jnp.sum(targets, axis=0)])


def local(hidden_states, head, labels):
    fsdp, vocab = (lax.axis_size("fsdp"), lax.axis_size("vocab"))
    f, v = (lax.axis_index("fsdp"), lax.axis_index("vocab"))
    features, width = head.shape
    tokens = hidden_states.shape[0]
    share = width // fsdp
    states = lax.all_gather(hidden_states.T, "fsdp", axis=1, tiled=True)
    states = lax.all_gather(states, "vocab", axis=0, tiled=True)
    wanted = lax.all_gather(labels, "fsdp", axis=0, tiled=True)
    weights = lax.all_to_all(head, "fsdp", split_axis=1, concat_axis=0, tiled=True)
    logits = lax.dot_general(
        weights, states, (((0,), (0,)), ((), ())), preferred_element_type=jnp.float32
    )
    rows = v * width + f * share + jnp.arange(share, dtype=jnp.int32)
    hits = rows[:, None] == wanted[None, :]
    local_target = jnp.sum(jnp.where(hits, logits, jnp.float32(0.0)), axis=0)
    local_peak = jnp.max(logits, axis=0)
    local_total = jnp.sum(jnp.exp(logits - local_peak[None, :]), axis=0)
    stats = jnp.stack([local_peak, local_total, local_target])
    stats = combine(lax.all_gather(stats, "fsdp", axis=0))
    stats = combine(lax.all_gather(stats, "vocab", axis=0))
    peak, total, target = (stats[0], stats[1], stats[2])
    loss = jnp.log(total) + peak - target
    token_loss = lax.dynamic_slice_in_dim(loss, f * tokens, tokens)
    errors = (jnp.exp(logits - peak[None, :]) / total[None, :] - hits.astype(jnp.float32)).astype(
        jnp.bfloat16
    )
    errors = lax.all_gather(errors, "fsdp", axis=0, tiled=True)
    terms = jnp.dot(head, errors, preferred_element_type=jnp.float32)
    parts = vocab // fsdp
    piece = features // parts
    terms = (
        terms.reshape(parts, piece, fsdp, tokens)
        .transpose(2, 0, 1, 3)
        .reshape(vocab, piece, tokens)
    )
    summed = lax.psum_scatter(terms, "vocab", scatter_dimension=0, tiled=False).astype(jnp.bfloat16)
    moves = [
        (a * vocab + u, u // parts * vocab + parts * a + u % parts)
        for a in range(fsdp)
        for u in range(vocab)
    ]
    state_grad = lax.ppermute(summed, ("fsdp", "vocab"), moves).T
    mine = lax.dynamic_slice_in_dim(states, f * features, features)
    head_grad = lax.dot_general(
        mine, errors, (((1,), (1,)), ((), ())), preferred_element_type=jnp.float32
    )
    return (token_loss, state_grad, head_grad)


def solution(mesh):
    in_specs = (P("fsdp", "vocab"), P("fsdp", "vocab"), P("fsdp"))
    out_specs = (P("fsdp"), P("fsdp", "vocab"), P("fsdp", "vocab"))
    return jax.shard_map(local, mesh=mesh, in_specs=in_specs, out_specs=out_specs, check_vma=False)
```

profile of v0, /device:TPU:17, one launch (start us, length us, event | category | flops | bytes accessed | tf_op | source)
XLA Modules:
  0.0 458.9 jit_solution(14088944663823949947)
XLA Ops:
  7.2 13.9 %all_gather.24 = bf16[96,1024]{1,0:T(8,128)(2,1)} all-gather(bf16[96,128]{1,0:T(8,128)(2,1)} %bitcast.67), channel_id=1, replica_groups=mesh['fsdp'=8,'vocab'=32] {'fsdp'}, dimensions={1}, use_global_device_ids=true | all-gather | bytes 221184 | tf_op jit(solution)/shard_map/all_gather | solution.py:20
  21.1 2.6 copy.18
  23.7 3.8 all-to-all-start
  27.5 24.3 %all-gather.2 = s32[8,1,128]{2,1,0:T(1,128)S(1)} all-gather(s32[1,1,128]{2,1,0:T(1,128)S(1)} %bitcast.73), channel_id=1, replica_groups=mesh['fsdp'=8,'vocab'=32] {'fsdp'}, dimensions={0}, use_global_device_ids=true | all-gather | bytes 4608 | tf_op jit(solution)/shard_map/all_gather | solution.py:22
  51.9 0.7 copy.19
  52.6 55.8 %all-gather.8.cloned.1.call-done = bf16[3072,1024]{1,0:T(8,128)(2,1)} async-done(((bf16[96,1024]{1,0:T(8,128)(2,1)}), bf16[3072,1024]{1,0:T(8,128)(2,1)}) %all-gather.8.cloned.1.call-update) | async-done | bytes 6291472 | tf_op jit(solution)/shard_map/all_gather | solution.py:21
  108.5 4.6 %fusion.15 = (f32[1024]{0:T(1024)S(1)}, f32[256,1024]{1,0:T(8,128)S(1)}) fusion(bf16[3072,256]{1,0:T(8,128)(2,1)S(1)} %bitcast.58, bf16[3072,1024]{1,0:T(8,128)(2,1)} %all-gather.8.cloned.1.call-done), kind=kOutput, calls=%fused_computation.32 | convolution fusion | flops 1610873856 | bytes 8916992 | tf_op jit(solution)/shard_map/dot_general | solution.py:24
  113.1 0.3 exponential_reduce_fusion
  113.3 14.5 %all-gather.3 = f32[8,3,1024]{2,1,0:T(4,128)S(1)} all-gather(f32[1,3,1024]{2,1,0:T(4,128)S(1)} %maximum_bitcast_fusion), channel_id=2, replica_groups=mesh['fsdp'=8,'vocab'=32] {'fsdp'}, dimensions={0}, use_global_device_ids=true | all-gather | bytes 110592 | tf_op jit(solution)/shard_map/all_gather | solution.py:33
  128.0 36.4 %all-gather.4 = f32[32,3,1024]{2,1,0:T(4,128)S(1)} all-gather(f32[1,3,1024]{2,1,0:T(4,128)S(1)} %maximum_bitcast_fusion.1), channel_id=3, replica_groups=mesh['fsdp'=8,'vocab'=32] {'vocab'}, dimensions={0}, use_global_device_ids=true | all-gather | bytes 405504 | tf_op jit(solution)/shard_map/all_gather | solution.py:34
  164.4 0.3 fusion.13
  164.8 1.1 fusion.2
  165.9 44.8 %all-gather.10.cloned.1.call-done = bf16[2048,1024]{1,0:T(8,128)(2,1)} async-done(((bf16[256,1024]{1,0:T(8,128)(2,1)}), bf16[2048,1024]{1,0:T(8,128)(2,1)}) %all-gather.10.cloned.1.call-update) | async-done | bytes 4194320 | tf_op jit(solution)/shard_map/all_gather | solution.py:41
  210.7 4.6 %convolution_bitcast_fusion = f32[384,1024]{0,1:T(8,128)S(1)} fusion(bf16[2048,1024]{1,0:T(8,128)(2,1)} %all-gather.10.cloned.1.call-done, bf16[384,2048]{1,0:T(8,128)(2,1)S(1)} %copy-done), kind=kOutput, calls=%fused_computation.1 | convolution fusion | flops 1610612736 | bytes 7340032 | tf_op jit(solution)/shard_map/dot_general | solution.py:42
  215.3 0.5 copy.22
  215.8 0.3 copy.29
  216.1 0.1 bitcast_bitcast_fusion
  216.3 1.4 copy.23
  217.7 0.6 dynamic_slice.6
  218.3 211.7 %reduce-scatter.2.cloned.1.call-done = f32[1,96,128]{2,1,0:T(8,128)} async-done(((f32[32,96,128]{2,1,0:T(8,128)}), f32[1,96,128]{2,1,0:T(8,128)}) %reduce-scatter.2.cloned.1.call-update) | async-done | bytes 49168 | tf_op jit(solution)/shard_map/reduce_scatter | solution.py:50
  430.0 0.8 convert_bitcast_fusion
  430.8 15.1 %collective-permute-start = (bf16[96,128]{1,0:T(8,128)(2,1)S(1)}, bf16[96,128]{1,0:T(8,128)(2,1)S(1)}, u32[]{:S(2)}, u32[]{:S(2)}) collective-permute-start(bf16[96,128]{1,0:T(8,128)(2,1)S(1)} %convert_bitcast_fusion), channel_id=1, source_target_pairs={{0,0},{1,1},{2,2},{3,3},{4,32},{5,33},{6,34},{7,35},{8,64},{9,65},... | collective-permute-start | bytes 73736 | tf_op jit(solution)/shard_map/ppermute | solution.py:56
  445.8 5.9 %fusion.3 = f32[384,2048]{1,0:T(8,128)} fusion(bf16[2048,1024]{1,0:T(8,128)(2,1)} %all-gather.10.cloned.1.call-done, bf16[3072,1024]{1,0:T(8,128)(2,1)} %all-gather.8.cloned.1.call-done, s32[]{:T(128)S(6)} %select_n.12), kind=kOutput, calls=%fused_computation.8 | convolution fusion | flops 1610612736 | bytes 8126468 | tf_op jit(solution)/shard_map/dot_general | solution.py:58
  451.8 0.6 copy.47
  (19 shorter events, 0.4 us)
Async XLA Ops:
  7.2 101.3 %all-gather.8.cloned.1.call-start = ((), (), s32[]{:S(2)}) async-start(), calls=%async_computation.2 | async-start | bytes 6488064 | tf_op jit(solution)/shard_map/all_gather | solution.py:21
  23.7 3.8 copy-start.1
  23.7 28.1 %all-to-all-start = ((bf16[384,8,256]{0,2,1:T(8,128)(2,1)}), bf16[384,8,256]{0,2,1:T(8,128)(2,1)S(1)}, u32[]{:S(2)}, u32[]{:S(2)}) async-start(bf16[384,8,256]{0,2,1:T(8,128)(2,1)} %bitcast), calls=%async_computation | async-start | bytes 3145728 | tf_op jit(solution)/shard_map/all_to_all | solution.py:23
  27.5 183.2 %all-gather.10.cloned.1.call-start = ((), (), s32[]{:S(2)}) async-start(), calls=%async_computation.3 | async-start | bytes 4718592 | tf_op jit(solution)/shard_map/all_gather | solution.py:41
  164.4 46.4 %copy-start = (bf16[384,2048]{1,0:T(8,128)(2,1)S(1)}, bf16[384,2048]{1,0:T(8,128)(2,1)}, u32[]{:S(2)}) copy-start(bf16[384,2048]{1,0:T(8,128)(2,1)} %param.4) | copy-start | bytes 4718596
  165.9 264.1 %reduce-scatter.2.cloned.1.call-start = ((), (), s32[]{:S(2)}) async-start(), calls=%async_computation.4 | async-start | bytes 1622016 | tf_op jit(solution)/shard_map/reduce_scatter | solution.py:50
  430.8 21.0 %collective-permute-start = (bf16[96,128]{1,0:T(8,128)(2,1)S(1)}, bf16[96,128]{1,0:T(8,128)(2,1)S(1)}, u32[]{:S(2)}, u32[]{:S(2)}) collective-permute-start(bf16[96,128]{1,0:T(8,128)(2,1)S(1)} %convert_bitcast_fusion), channel_id=1, source_target_pairs={{0,0},{1,1},{2,2},{3,3},{4,32},{5,33},{6,34},{7,35},{8,64},{9,65},... | collective-permute-start | bytes 73736 | tf_op jit(solution)/shard_map/ppermute | solution.py:56
Sparse Core Ops, SparseCore 0:
  21.3 87.1 all-gather.7
  166.0 44.6 all-gather.9
  217.8 212.0 reduce-scatter.1
where the time goes:
time: 459 us
  waiting for transfers between devices  312 us (68%)
  blocking collectives  89.1 us (19%)
  starting transfers between devices  18.9 us (4%)
  matrix products  15.1 us (3%)
  between operations  13.8 us (3%)
  local copies, waits for them, and re-layouts  6.86 us (1%)
    reduce_scatter x1, waiting for transfers between devices, local(): lax.psum_scatter(terms, 'vocab', scatter_dimension=0, tiled=False)  212 us
    all_gather x1, waiting for transfers between devices, local(): states = lax.all_gather(states, 'vocab', axis=0, tiled=True)  55.8 us
    all_gather x1, waiting for transfers between devices, local(): errors = lax.all_gather(errors, 'fsdp', axis=0, tiled=True)  44.8 us
    all_gather x1, blocking collectives, local(): stats = combine(lax.all_gather(stats, 'vocab', axis=0))  36.4 us
    all_gather x1, blocking collectives, local(): wanted = lax.all_gather(labels, 'fsdp', axis=0, tiled=True)  24.3 us
    ppermute x1, starting transfers between devices, local(): state_grad = lax.ppermute(summed, ('fsdp', 'vocab'), moves).T  15.1 us
    all_gather x1, blocking collectives, local(): stats = combine(lax.all_gather(stats, 'fsdp', axis=0))  14.5 us
    all_gather x1, blocking collectives, local(): states = lax.all_gather(hidden_states.T, 'fsdp', axis=1, tiled=True)  13.9 us
  transfers between devices with their start and end apart: 5, of which 3 were waited for; matrix products, arithmetic and copies ran while one was open for 2% of the time, Pallas kernels for 0%

commit v1 on v0

--- a/solution.py
+++ b/solution.py
@@ -2,6 +2,7 @@
 import jax.numpy as jnp
 from jax import lax
 from jax.sharding import PartitionSpec as P
+from jax.lax import all_to_all, axis_size
 
 
 def combine(stats):
@@ -18,7 +19,13 @@
     tokens = hidden_states.shape[0]
     share = width // fsdp
     states = lax.all_gather(hidden_states.T, "fsdp", axis=1, tiled=True)
-    states = lax.all_gather(states, "vocab", axis=0, tiled=True)
+    right_arr = all_to_all(
+        jnp.stack([states for _ in range(axis_size("vocab"))]),
+        axis_name="vocab",
+        split_axis=0,
+        concat_axis=0,
+    )
+    states = jnp.concatenate(right_arr, axis=0)
     wanted = lax.all_gather(labels, "fsdp", axis=0, tiled=True)
     weights = lax.all_to_all(head, "fsdp", split_axis=1, concat_axis=0, tiled=True)
     logits = lax.dot_general(

time: 459 us -> 549 us (1.20)
  waiting for transfers between devices: 312 us -> 387 us
  starting transfers between devices: 18.9 us -> 31.6 us
    all_to_all x0 -> x1, waiting for transfers between devices: none -> 131 us  [local(): all_to_all(jnp.stack([states for _ in range(axis_size('vocab'))]), axis_n...]
    all_gather x1 -> x0, waiting for transfers between devices: 55.8 us -> none  [local(): states = lax.all_gather(states, 'vocab', axis=0, tiled=True)]
    all_gather x1, blocking collectives: 24.3 us -> 10 us  [local(): wanted = lax.all_gather(labels, 'fsdp', axis=0, tiled=True)]
    all_gather x1, blocking collectives: 13.9 us -> 27 us  [local(): states = lax.all_gather(hidden_states.T, 'fsdp', axis=1, tiled=True)]
    all_to_all x0 -> x1, starting transfers between devices: none -> 11.2 us  [local(): all_to_all(jnp.stack([states for _ in range(axis_size('vocab'))]), axis_n...]
  transfers between devices with their start and end apart: 5 -> 5, of which waited for: 3 -> 3; matrix products, arithmetic and copies ran while one was open for 2% -> 1% of each run, Pallas kernels for 0% -> 0%
where the time goes in v1:
time: 549 us
  waiting for transfers between devices  387 us (70%)
  blocking collectives  88.2 us (16%)
  starting transfers between devices  31.6 us (6%)
  matrix products  15.2 us (3%)
  between operations  14.2 us (3%)
  local copies, waits for them, and re-layouts  10.3 us (2%)
    reduce_scatter x1, waiting for transfers between devices, local(): lax.psum_scatter(terms, 'vocab', scatter_dimension=0, tiled=False)  212 us
    all_to_all x1, waiting for transfers between devices, local(): all_to_all(jnp.stack([states for _ in range(axis_size('vocab'))]), axis_n...  131 us
    all_gather x1, waiting for transfers between devices, local(): errors = lax.all_gather(errors, 'fsdp', axis=0, tiled=True)  44.5 us
    all_gather x1, blocking collectives, local(): stats = combine(lax.all_gather(stats, 'vocab', axis=0))  37.4 us
    all_gather x1, blocking collectives, local(): states = lax.all_gather(hidden_states.T, 'fsdp', axis=1, tiled=True)  27 us
    ppermute x1, starting transfers between devices, local(): state_grad = lax.ppermute(summed, ('fsdp', 'vocab'), moves).T  15.2 us
    all_gather x1, blocking collectives, local(): stats = combine(lax.all_gather(stats, 'fsdp', axis=0))  13.9 us
    all_to_all x1, starting transfers between devices, local(): all_to_all(jnp.stack([states for _ in range(axis_size('vocab'))]), axis_n...  11.2 us
  transfers between devices with their start and end apart: 5, of which 3 were waited for; matrix products, arithmetic and copies ran while one was open for 1% of the time, Pallas kernels for 0%

profile of v1, /device:TPU:17, one launch (start us, length us, event | category | flops | bytes accessed | tf_op | source)
XLA Modules:
  0.0 548.8 jit_solution(15614455325541410461)
XLA Ops:
  7.2 2.6 copy.18
  9.7 5.1 all-to-all-start
  14.9 27.0 %all_gather.21 = bf16[96,1024]{1,0:T(8,128)(2,1)S(1)} all-gather(bf16[96,128]{1,0:T(8,128)(2,1)S(1)} %bitcast.68), channel_id=1, replica_groups=mesh['fsdp'=8,'vocab'=32] {'fsdp'}, dimensions={1}, use_global_device_ids=true | all-gather | bytes 221184 | tf_op jit(solution)/shard_map/all_gather | solution.py:21
  41.8 3.5 stack.18
  45.3 11.2 %all-to-all-start.1 = ((bf16[32,96,1024]{2,1,0:T(8,128)(2,1)}), bf16[32,96,1024]{2,1,0:T(8,128)(2,1)}, u32[]{:S(2)}, u32[]{:S(2)}) async-start(bf16[32,96,1024]{2,1,0:T(8,128)(2,1)} %stack.18), calls=%async_computation.1 | async-start | bytes 12582912 | tf_op jit(solution)/shard_map/all_to_all | solution.py:22
  56.6 10.0 %all-gather.2 = s32[8,1,128]{2,1,0:T(1,128)S(1)} all-gather(s32[1,1,128]{2,1,0:T(1,128)S(1)} %bitcast.74), channel_id=1, replica_groups=mesh['fsdp'=8,'vocab'=32] {'fsdp'}, dimensions={0}, use_global_device_ids=true | all-gather | bytes 4608 | tf_op jit(solution)/shard_map/all_gather | solution.py:29
  66.6 0.7 copy.19
  67.3 130.6 %all-to-all-done.1 = bf16[32,96,1024]{2,1,0:T(8,128)(2,1)} async-done(((bf16[32,96,1024]{2,1,0:T(8,128)(2,1)}), bf16[32,96,1024]{2,1,0:T(8,128)(2,1)}, u32[]{:S(2)}, u32[]{:S(2)}) %all-to-all-start.1) | async-done | bytes 6291488 | tf_op jit(solution)/shard_map/all_to_all | solution.py:22
  197.9 4.6 fusion.15
  202.9 13.9 %all-gather.3 = f32[8,3,1024]{2,1,0:T(4,128)S(1)} all-gather(f32[1,3,1024]{2,1,0:T(4,128)S(1)} %maximum_bitcast_fusion), channel_id=2, replica_groups=mesh['fsdp'=8,'vocab'=32] {'fsdp'}, dimensions={0}, use_global_device_ids=true | all-gather | bytes 110592 | tf_op jit(solution)/shard_map/all_gather | solution.py:40
  216.9 37.4 %all-gather.4 = f32[32,3,1024]{2,1,0:T(4,128)S(1)} all-gather(f32[1,3,1024]{2,1,0:T(4,128)S(1)} %maximum_bitcast_fusion.1), channel_id=3, replica_groups=mesh['fsdp'=8,'vocab'=32] {'vocab'}, dimensions={0}, use_global_device_ids=true | all-gather | bytes 405504 | tf_op jit(solution)/shard_map/all_gather | solution.py:41
  254.3 0.3 fusion.13
  254.7 1.1 fusion.2
  255.8 44.5 %all-gather.7.cloned.1.call-done = bf16[2048,1024]{1,0:T(8,128)(2,1)} async-done(((bf16[256,1024]{1,0:T(8,128)(2,1)}), bf16[2048,1024]{1,0:T(8,128)(2,1)}) %all-gather.7.cloned.1.call-update) | async-done | bytes 4194320 | tf_op jit(solution)/shard_map/all_gather | solution.py:48
  300.3 4.6 convolution_bitcast_fusion
  304.9 0.5 copy.22
  305.4 0.3 copy.29
  305.9 1.4 copy.23
  307.3 0.6 dynamic_slice.6
  307.9 211.5 %reduce-scatter.2.cloned.1.call-done = f32[1,96,128]{2,1,0:T(8,128)} async-done(((f32[32,96,128]{2,1,0:T(8,128)}), f32[1,96,128]{2,1,0:T(8,128)}) %reduce-scatter.2.cloned.1.call-update) | async-done | bytes 49168 | tf_op jit(solution)/shard_map/reduce_scatter | solution.py:57
  519.5 0.8 convert_bitcast_fusion
  520.3 15.2 %collective-permute-start = (bf16[96,128]{1,0:T(8,128)(2,1)S(1)}, bf16[96,128]{1,0:T(8,128)(2,1)S(1)}, u32[]{:S(2)}, u32[]{:S(2)}) collective-permute-start(bf16[96,128]{1,0:T(8,128)(2,1)S(1)} %convert_bitcast_fusion), channel_id=1, source_target_pairs={{0,0},{1,1},{2,2},{3,3},{4,32},{5,33},{6,34},{7,35},{8,64},{9,65},... | collective-permute-start | bytes 73736 | tf_op jit(solution)/shard_map/ppermute | solution.py:63
  535.5 5.9 %fusion.3 = f32[384,2048]{1,0:T(8,128)} fusion(bf16[2048,1024]{1,0:T(8,128)(2,1)} %all-gather.7.cloned.1.call-done, bf16[3072,1024]{1,0:T(8,128)(2,1)} %bitcast.4, s32[]{:T(128)S(6)} %select_n.12), kind=kOutput, calls=%fused_computation.8 | convolution fusion | flops 1610612736 | bytes 8126468 | tf_op jit(solution)/shard_map/dot_general | solution.py:65
  541.4 0.6 copy.47
  (21 shorter events, 0.7 us)
Async XLA Ops:
  9.7 5.1 copy-start.1
  9.7 32.1 %all-to-all-start = ((bf16[384,8,256]{0,2,1:T(8,128)(2,1)}), bf16[384,8,256]{0,2,1:T(8,128)(2,1)S(1)}, u32[]{:S(2)}, u32[]{:S(2)}) async-start(bf16[384,8,256]{0,2,1:T(8,128)(2,1)} %bitcast), calls=%async_computation | async-start | bytes 3145728 | tf_op jit(solution)/shard_map/all_to_all | solution.py:30
  45.3 11.3 %copy-start.2 = (s32[128]{0:T(128)S(1)}, s32[128]{0:T(128)}, u32[]{:S(2)}) copy-start(s32[128]{0:T(128)} %param.5) | copy-start | bytes 1540
  45.3 152.7 %all-to-all-start.1 = ((bf16[32,96,1024]{2,1,0:T(8,128)(2,1)}), bf16[32,96,1024]{2,1,0:T(8,128)(2,1)}, u32[]{:S(2)}, u32[]{:S(2)}) async-start(bf16[32,96,1024]{2,1,0:T(8,128)(2,1)} %stack.18), calls=%async_computation.1 | async-start | bytes 12582912 | tf_op jit(solution)/shard_map/all_to_all | solution.py:22
  56.5 243.8 %all-gather.7.cloned.1.call-start = ((), (), s32[]{:S(2)}) async-start(), calls=%async_computation.3 | async-start | bytes 4718592 | tf_op jit(solution)/shard_map/all_gather | solution.py:48
  254.3 46.0 %copy-start = (bf16[384,2048]{1,0:T(8,128)(2,1)S(1)}, bf16[384,2048]{1,0:T(8,128)(2,1)}, u32[]{:S(2)}) copy-start(bf16[384,2048]{1,0:T(8,128)(2,1)} %param.4) | copy-start | bytes 4718596
  255.8 263.7 %reduce-scatter.2.cloned.1.call-start = ((), (), s32[]{:S(2)}) async-start(), calls=%async_computation.4 | async-start | bytes 1622016 | tf_op jit(solution)/shard_map/reduce_scatter | solution.py:57
  520.3 21.1 %collective-permute-start = (bf16[96,128]{1,0:T(8,128)(2,1)S(1)}, bf16[96,128]{1,0:T(8,128)(2,1)S(1)}, u32[]{:S(2)}, u32[]{:S(2)}) collective-permute-start(bf16[96,128]{1,0:T(8,128)(2,1)S(1)} %convert_bitcast_fusion), channel_id=1, source_target_pairs={{0,0},{1,1},{2,2},{3,3},{4,32},{5,33},{6,34},{7,35},{8,64},{9,65},... | collective-permute-start | bytes 73736 | tf_op jit(solution)/shard_map/ppermute | solution.py:63
Sparse Core Ops, SparseCore 0:
  255.9 44.3 all-gather.6
  307.4 211.9 reduce-scatter.1
